TPU v7x, 256 devices: a whole 4x4x8 slice. The times are simulated.
256 devices in a mesh: ctx: 32 (over x, y, core), tp: 8 (over z).
Axes of the slice: x: 4, y: 4, z: 8, core: 2. Of those that a mesh axis runs over, the one named last changes fastest.
Arguments:
- patches: bfloat16 [16384, 1280], P('ctx'), may hold values from -21 to 21
- window_ids: int32 [16384], P('ctx'), may hold values from -1 to 4095, as said below
- positions: int32 [4096], P('ctx'), may hold values from 0 to 32768, as said below
- text_embed: bfloat16 [32768, 8192], P('ctx', 'tp'), may hold values from -6 to 6
- cotangent: bfloat16 [32768, 8192], P('ctx', 'tp'), may hold values from -0.119628906 to 0.119628906
- qkv_weight: bfloat16 [3, 1280, 1280], P(None, None, 'tp'), may hold values from -0.15625 to 0.15625
- out_weight: bfloat16 [1280, 1280], P('tp'), may hold values from -0.15625 to 0.15625
- merger_weight: bfloat16 [5120, 8192], P('ctx', 'tp'), may hold values from -0.078125 to 0.078125
- norm_gain: bfloat16 [8192], P('tp'), may hold values from 0.099609375 to 1.8984375
Outputs:
- normed: bfloat16 [32768, 8192], P('ctx', 'tp')
- merger_grad: float32 [5120, 8192], P('ctx', 'tp')
Inputs may be any that keep to these rules, and one draw needn't show every extreme that they name: `window_ids`: windows are runs of consecutive patch slots of one index of ctx, each of 4 to 64 slots and a multiple of 4; every window id belongs to one index of ctx; the padding slots of an index of ctx come after its live slots and carry -1. Merged slot j of an index of ctx covers its patch slots 4j to 4j+3 and is live exactly when those are; live slots carry distinct positions, dead ones carry 32768. The live slots of one index of ctx name at most 4 positions among the 1024 positions of any one index of ctx.
All inputs are finite; a program needn't handle non-finite values.
Results may differ from a plain program's by a relative error of at most 0.014.
Values may be sent and summed in bfloat16 or wider, within the bound.
A program may use at most 128 MiB of HBM per device.

v0:
```python
import jax
import jax.numpy as jnp
from jax import lax
from jax.sharding import PartitionSpec as P

D = 8192
HEAD_DIM = 80


def sent_to_all(shard, axis):
    copies = jnp.broadcast_to(shard, (lax.axis_size(axis), *shard.shape))
    return lax.all_to_all(copies, axis, split_axis=0, concat_axis=0, tiled=True)


def taken_together(shard, axis):
    return sent_to_all(shard, axis).sum(axis=0)


def in_one(arrays, axis):
    ends = [0]
    for a in arrays:
        ends.append(ends[-1] + a.size)
    so_far = taken_together(jnp.concatenate([a.ravel() for a in arrays]), axis)
    return tuple((so_far[b:e].reshape(a.shape) for a, b, e in zip(arrays, ends, ends[1:])))


def window_attention(patches, window_ids, qkv_weight):
    slot_rows = patches.shape[0]
    projected = [
        jnp.dot(patches, qkv_weight[i], preferred_element_type=jnp.float32).astype(jnp.bfloat16)
        for i in range(3)
    ]
    local_heads = qkv_weight.shape[2] // HEAD_DIM
    queries = projected[0].reshape(slot_rows, local_heads, HEAD_DIM)
    keys_all = projected[1].reshape(slot_rows, local_heads, HEAD_DIM)
    values = projected[2].reshape(slot_rows, local_heads, HEAD_DIM)
    width = min(512, slot_rows)
    factor = 1.0 / HEAD_DIM**0.5

    def one_block(block_index):
        scores = (
            jnp.einsum("qhd,khd->hqk", queries, keys_all, preferred_element_type=jnp.float32)
            * factor
        )
        allowed = (window_ids[:, None] == window_ids[None, :]) & (window_ids[None, :] >= 0)
        scores = jnp.where(allowed[None], scores, jnp.float32(-1e30))
        highest = jnp.max(scores, axis=2, keepdims=True)
        weights = jnp.exp(scores - highest)
        probs = (weights / jnp.sum(weights, axis=2, keepdims=True)).astype(jnp.bfloat16)
        attended = jnp.einsum("hqk,khd->qhd", probs, values, preferred_element_type=jnp.float32)
        return attended.astype(jnp.bfloat16).reshape(width, local_heads * HEAD_DIM)

    blocks = lax.map(one_block, jnp.arange(slot_rows // width, dtype=jnp.int32))
    return blocks.reshape(slot_rows, local_heads * HEAD_DIM)


def contract_rows(left, right):
    return lax.dot_general(
        left, right, (((0,), (0,)), ((), ())), preferred_element_type=jnp.float32
    )


def shards(
    patches,
    window_ids,
    positions,
    text_embed,
    cotangent,
    qkv_weight,
    out_weight,
    merger_weight,
    norm_gain,
):
    ctx_size = lax.axis_size("ctx")
    slots = positions.shape[0]
    tok_rows = text_embed.shape[0]
    bucket_size = slots // ctx_size
    attended = window_attention(patches, window_ids, qkv_weight)
    partial_out = jnp.dot(attended, out_weight, preferred_element_type=jnp.float32)
    summed = lax.psum(partial_out.astype(jnp.bfloat16), "tp").astype(jnp.float32)
    hidden = (patches.astype(jnp.float32) + summed).astype(jnp.bfloat16)
    merged_in = hidden.reshape(slots, 4 * hidden.shape[1])
    columns = lax.all_to_all(merged_in, "ctx", split_axis=1, concat_axis=0, tiled=True)
    chosen = merged_in
    merged = jnp.dot(
        chosen,
        lax.all_gather(merger_weight, "ctx", axis=0, tiled=True),
        preferred_element_type=jnp.float32,
    ).astype(jnp.bfloat16)
    target = positions // tok_rows
    hits = (target[:, None] == jnp.arange(ctx_size, dtype=jnp.int32)[None, :]).astype(jnp.int32)
    ranks = jnp.sum(jnp.cumsum(hits, axis=0) * hits, axis=1) - 1
    bucket = jnp.where(target < ctx_size, target * bucket_size + ranks, -1)
    select = jnp.arange(slots, dtype=jnp.int32)[:, None] == bucket[None, :]
    select_mat = select.astype(jnp.bfloat16)
    outgoing = jnp.dot(select_mat, merged, preferred_element_type=jnp.float32).astype(jnp.bfloat16)
    local_row = positions % tok_rows
    occupied = jnp.any(select, axis=1)
    out_rows = jnp.where(occupied, jnp.sum(jnp.where(select, local_row[None, :], 0), axis=1), -1)
    incoming, in_rows = (
        lax.all_to_all(outgoing, "ctx", split_axis=0, concat_axis=0, tiled=True),
        lax.all_to_all(out_rows, "ctx", split_axis=0, concat_axis=0, tiled=True),
    )
    placed = jnp.arange(tok_rows, dtype=jnp.int32)[:, None] == in_rows[None, :]
    placed_mat = placed.astype(jnp.bfloat16)
    vision = jnp.dot(placed_mat, incoming, preferred_element_type=jnp.float32)
    is_vision = jnp.any(placed, axis=1)
    embedded = jnp.where(is_vision[:, None], vision, text_embed.astype(jnp.float32))
    gain_vec = norm_gain.astype(jnp.float32)[None, :]
    gained = gain_vec * cotangent.astype(jnp.float32)
    squares, inner = in_one(
        (jnp.sum(embedded * embedded, axis=1), jnp.sum(embedded * gained, axis=1)), "tp"
    )
    scale = lax.rsqrt(squares / D + 1e-06)[:, None]
    normed = (embedded * scale * gain_vec).astype(jnp.bfloat16)
    d_embed = (scale * gained - embedded * scale**3 * inner[:, None] / D).astype(jnp.bfloat16)
    back_rows = contract_rows(placed_mat, d_embed).astype(jnp.bfloat16)
    returned = lax.all_to_all(back_rows, "ctx", split_axis=0, concat_axis=0, tiled=True)
    d_merged = contract_rows(select_mat, returned).astype(jnp.bfloat16)
    chosen = columns
    merger_grad = contract_rows(chosen, lax.all_gather(d_merged, "ctx", axis=0, tiled=True))
    return (normed, merger_grad)


def solution(mesh):
    in_specs = (
        P("ctx", None),
        P("ctx"),
        P("ctx"),
        P("ctx", "tp"),
        P("ctx", "tp"),
        P(None, None, "tp"),
        P("tp", None),
        P("ctx", "tp"),
        P("tp"),
    )
    out_specs = (P("ctx", "tp"), P("ctx", "tp"))
    return jax.shard_map(shards, mesh=mesh, in_specs=in_specs, out_specs=out_specs, check_vma=False)
```

profile of v0, /device:TPU:1, one launch (start us, length us, event | category | flops | bytes accessed | tf_op | source)
XLA Modules:
  0.0 239.2 jit_solution(6177392035362610401)
XLA Ops:
  8.1 2.1 convolution_convert_fusion.7
  10.2 2.0 convolution_convert_fusion.5
  12.2 1.6 convolution_convert_fusion.6
  15.0 1.2 convolution_convert_fusion.4
  16.3 1.6 convolution_convert_fusion
  19.9 8.6 %all-to-all-start = ((s32[32,4,1]{1,2,0:T(1,128)}), s32[32,4,1]{1,2,0:T(1,128)S(1)}, u32[]{:S(2)}, u32[]{:S(2)}) async-start(s32[32,4,1]{1,2,0:T(1,128)} %bitcast), calls=%async_computation | async-start | bytes 32768 | tf_op jit(solution)/shard_map/all_to_all | solution.py:102
  28.5 66.8 %all-reduce.2.cloned.1.call-done = bf16[512,1280]{1,0:T(8,128)(2,1)} async-done(((bf16[512,1280]{1,0:T(8,128)(2,1)}), bf16[512,1280]{1,0:T(8,128)(2,1)}) %all-reduce.2.cloned.1.call-update) | async-done | bytes 1310736 | tf_op jit(solution)/shard_map/psum | solution.py:80
  95.3 1.6 add_convert_fusion
  97.8 5.7 %convolution_convert_fusion.2 = bf16[128,1024]{1,0:T(8,128)(2,1)S(1)} fusion(bf16[128,5120]{1,0:T(8,128)(2,1)S(1)} %reshape.118, bf16[5120,1024]{1,0:T(8,128)(2,1)} %all-gather.3.cloned.1.call-done, s32[128]{0:T(128)S(1)} %compare_select_fusion), kind=kOutput, calls=%fused_computation.19 | convolution fusion | flops 1376010240 | bytes 12059136 | tf_op jit(solution)/shard_map/dot_general | solution.py:96
  104.3 11.4 %all-to-all-start.1 = ((bf16[32,4,1024]{2,1,0:T(4,128)(2,1)}), bf16[32,4,1024]{2,1,0:T(4,128)(2,1)S(1)}, u32[]{:S(2)}, u32[]{:S(2)}) async-start(bf16[32,4,1024]{2,1,0:T(4,128)(2,1)} %all_to_all.39), calls=%async_computation.1 | async-start | bytes 524288 | tf_op jit(solution)/shard_map/all_to_all | solution.py:101
  115.8 3.9 %copy.37 = bf16[1024,1024]{0,1:T(8,128)(2,1)} copy(bf16[1024,1024]{1,0:T(8,128)(2,1)} %param.13) | data formatting | bytes 4194304 | tf_op args[4]
  119.7 4.0 %copy.36 = bf16[1024,1024]{0,1:T(8,128)(2,1)} copy(bf16[1024,1024]{1,0:T(8,128)(2,1)} %param.12) | data formatting | bytes 4194304 | tf_op args[3]
  125.2 5.6 %multiply_reduce_fusion.1 = (f32[1024]{0:T(1024)S(1)}, f32[1024]{0:T(1024)S(1)}, f32[1024,1024]{0,1:T(8,128)}) fusion(bf16[1024,1024]{0,1:T(8,128)(2,1)} %copy.37, f32[1024]{0:T(1024)S(1)} %convert_element_type.78, bf16[1024,1024]{0,1:T(8,128)(2,1)} %copy.36, bf16[128,1024]{1,0:T(8,128)(2,1)S(1)} %all_to_all.41, s32[128]{0:T(128)S(1)} %eq.74, ...), kind=kOutput, calls=%fused_computation.5 | convolution fusion | flops 276953088 | bytes 8664576 | tf_op jit(solution)/shard_map/dot_general | solution.py:106
  130.9 11.2 %all_to_all.55 = f32[8,1,2048]{2,1,0:T(1,128)S(1)} all-to-all(f32[8,1,2048]{2,1,0:T(1,128)S(1)} %broadcast_in_dim.73), channel_id=1, replica_groups=mesh['ctx'=32,'tp'=8] {'tp'}, dimensions={0} | all-to-all | bytes 131072 | tf_op jit(solution)/shard_map/all_to_all | solution.py:12
  142.2 4.3 %fusion.6 = bf16[128,1024]{1,0:T(8,128)(2,1)S(1)} fusion(f32[1024,1024]{0,1:T(8,128)} %get-tuple-element.37, bf16[1024,1024]{0,1:T(8,128)(2,1)} %copy.37, f32[1024]{0:T(1024)S(1)} %get-tuple-element.34, f32[1024]{0:T(1024)S(1)} %get-tuple-element.32, f32[1024]{0:T(1024)S(1)} %get-tuple-element.33, f32[1024]{0:T(1024)S(1)} %convert_element_type.78, ...), kind=kOutput, calls=%fused_computation.17 | convolution fusion | flops 277217280 | bytes 6570496 | tf_op jit(solution)/shard_map/dot_general | solution.py:58
  146.5 17.6 %all_to_all.56 = bf16[32,4,1024]{2,1,0:T(4,128)(2,1)S(1)} all-to-all(bf16[32,4,1024]{2,1,0:T(4,128)(2,1)S(1)} %all_to_all.47), channel_id=1, replica_groups=mesh['ctx'=32,'tp'=8] {'ctx'}, dimensions={0} | all-to-all | bytes 524288 | tf_op jit(solution)/shard_map/all_to_all | solution.py:118
  165.2 3.6 %all_to_all.43 = bf16[128,32,160]{2,1,0:T(8,128)(2,1)} reshape(bf16[512,1280]{1,0:T(8,128)(2,1)S(1)} %add_convert_fusion) | data formatting | bytes 2621440 | tf_op jit(solution)/shard_map/all_to_all | solution.py:83
  168.8 4.4 %copy.39 = bf16[128,32,160]{0,2,1:T(8,128)(2,1)} copy(bf16[128,32,160]{2,1,0:T(8,128)(2,1)} %all_to_all.43) | data formatting | bytes 2621440 | tf_op jit(solution)/shard_map/all_to_all | solution.py:83
  173.2 4.5 %all-to-all-start.3 = ((bf16[128,32,160]{0,2,1:T(8,128)(2,1)}), bf16[128,32,160]{0,2,1:T(8,128)(2,1)}, u32[]{:S(2)}, u32[]{:S(2)}) async-start(bf16[128,32,160]{0,2,1:T(8,128)(2,1)} %copy.39), calls=%async_computation.3 | async-start | bytes 2621440 | tf_op jit(solution)/shard_map/all_to_all | solution.py:83
  177.7 2.6 %multiply_convert_fusion = bf16[1024,1024]{0,1:T(8,128)(2,1)S(1)} fusion(f32[1024,1024]{0,1:T(8,128)} %get-tuple-element.37, f32[1024]{0:T(1024)S(1)} %get-tuple-element.33, f32[1024]{0:T(1024)S(1)} %convert_element_type.78), kind=kLoop, calls=%fused_computation.2 | loop fusion | flops 3145728 | bytes 6299648 | tf_op jit(solution)/shard_map/convert_element_type | solution.py:115
  180.3 2.6 %copy.41 = bf16[1024,1024]{1,0:T(8,128)(2,1)} copy(bf16[1024,1024]{0,1:T(8,128)(2,1)S(1)} %multiply_convert_fusion) | data formatting | bytes 4194304
  182.9 15.3 %all-to-all-done.3 = bf16[128,32,160]{0,2,1:T(8,128)(2,1)} async-done(((bf16[128,32,160]{0,2,1:T(8,128)(2,1)}), bf16[128,32,160]{0,2,1:T(8,128)(2,1)}, u32[]{:S(2)}, u32[]{:S(2)}) %all-to-all-start.3) | async-done | bytes 1310752 | tf_op jit(solution)/shard_map/all_to_all | solution.py:83
  198.2 27.4 %all-gather.5.cloned.1.call-done = bf16[4096,1024]{1,0:T(8,128)(2,1)} async-done(((bf16[128,1024]{1,0:T(8,128)(2,1)}), bf16[4096,1024]{1,0:T(8,128)(2,1)}) %all-gather.5.cloned.1.call-update) | async-done | bytes 8388624 | tf_op jit(solution)/shard_map/all_gather | solution.py:121
  225.6 6.2 %fusion.3 = f32[160,1024]{1,0:T(8,128)} fusion(bf16[4096,1024]{1,0:T(8,128)(2,1)} %all-gather.5.cloned.1.call-done, bf16[128,32,160]{0,2,1:T(8,128)(2,1)} %all-to-all-done.3), kind=kOutput, calls=%fused_computation.14 | convolution fusion | flops 1342177280 | bytes 10354688 | tf_op jit(solution)/shard_map/dot_general | solution.py:58
  (46 shorter events, 7.8 us)
Async XLA Ops:
  8.0 8.3 %copy-start = (bf16[160,1280]{1,0:T(8,128)(2,1)S(1)}, bf16[160,1280]{1,0:T(8,128)(2,1)}, u32[]{:S(2)}) copy-start(bf16[160,1280]{1,0:T(8,128)(2,1)} %param.15) | copy-start | bytes 1228804
  8.0 4.1 %copy-start.1 = (bf16[512,1280]{1,0:T(8,128)(2,1)S(1)}, bf16[512,1280]{1,0:T(8,128)(2,1)}, u32[]{:S(2)}) copy-start(bf16[512,1280]{1,0:T(8,128)(2,1)} %param.9) | copy-start | bytes 3932164
  8.0 87.3 %all-reduce.2.cloned.1.call-start = ((), (), s32[]{:S(2)}) async-start(), calls=%async_computation.5 | async-start | bytes 2621440 | tf_op jit(solution)/shard_map/psum | solution.py:80
  10.2 3.6 %copy-start.2 = (s32[512]{0:T(512)S(1)}, s32[512]{0:T(512)}, u32[]{:S(2)}) copy-start(s32[512]{0:T(512)} %param.10) | copy-start | bytes 6148
  16.2 2.2 copy-start.4
  17.9 79.9 %all-gather.3.cloned.1.call-start = ((), (), s32[]{:S(2)}) async-start(), calls=%async_computation.6 | async-start | bytes 10813440 | tf_op jit(solution)/shard_map/all_gather | solution.py:87
  19.9 84.4 %all-to-all-start = ((s32[32,4,1]{1,2,0:T(1,128)}), s32[32,4,1]{1,2,0:T(1,128)S(1)}, u32[]{:S(2)}, u32[]{:S(2)}) async-start(s32[32,4,1]{1,2,0:T(1,128)} %bitcast), calls=%async_computation | async-start | bytes 32768 | tf_op jit(solution)/shard_map/all_to_all | solution.py:102
  97.8 18.0 %copy-start.3 = (bf16[1024]{0:T(1024)(128)(2,1)S(1)}, bf16[1024]{0:T(1024)(128)(2,1)}, u32[]{:S(2)}) copy-start(bf16[1024]{0:T(1024)(128)(2,1)} %param.17) | copy-start | bytes 6148
  104.3 20.9 %all-to-all-start.1 = ((bf16[32,4,1024]{2,1,0:T(4,128)(2,1)}), bf16[32,4,1024]{2,1,0:T(4,128)(2,1)S(1)}, u32[]{:S(2)}, u32[]{:S(2)}) async-start(bf16[32,4,1024]{2,1,0:T(4,128)(2,1)} %all_to_all.39), calls=%async_computation.1 | async-start | bytes 524288 | tf_op jit(solution)/shard_map/all_to_all | solution.py:101
  115.7 109.9 %all-gather.5.cloned.1.call-start = ((), (), s32[]{:S(2)}) async-start(), calls=%async_computation.7 | async-start | bytes 8650752 | tf_op jit(solution)/shard_map/all_gather | solution.py:121
  173.2 25.0 %all-to-all-start.3 = ((bf16[128,32,160]{0,2,1:T(8,128)(2,1)}), bf16[128,32,160]{0,2,1:T(8,128)(2,1)}, u32[]{:S(2)}, u32[]{:S(2)}) async-start(bf16[128,32,160]{0,2,1:T(8,128)(2,1)} %copy.39), calls=%async_computation.3 | async-start | bytes 2621440 | tf_op jit(solution)/shard_map/all_to_all | solution.py:83
Sparse Core Ops, SparseCore 0:
  18.0 77.2 all-reduce.1
Sparse Core Ops, SparseCore 1:
  20.9 66.7 all-gather.2
  165.3 60.3 all-gather.4
where the time goes:
time: 240 us; the launch traced here: 239 us
  waiting for transfers between devices  110 us (46%)
  matrix products  32.1 us (13%)
  blocking collectives  28.8 us (12%)
  starting transfers between devices  24.6 us (10%)
  local copies, waits for them, and re-layouts  21.8 us (9%)
  between operations  15.8 us (7%)
  other arithmetic  6.13 us (3%)
    psum x1, waiting for transfers between devices, shards(): lax.psum(partial_out.astype(jnp.bfloat16), 'tp').astype(jnp.float32)  66.8 us
    all_gather x1, waiting for transfers between devices, shards(): lax.all_gather(d_merged, 'ctx', axis=0, tiled=True)  27.4 us
    all_to_all x1, blocking collectives, shards(): lax.all_to_all(back_rows, 'ctx', split_axis=0, concat_axis=0, tiled=True)  17.6 us
    all_to_all x1, waiting for transfers between devices, shards(): lax.all_to_all(merged_in, 'ctx', split_axis=1, concat_axis=0, tiled=True)  15.3 us
    all_to_all x1, starting transfers between devices, shards(): lax.all_to_all(outgoing, 'ctx', split_axis=0, concat_axis=0, tiled=True)  11.4 us
    dot_general x3, matrix products, contract_rows(): lax.dot_general(left, right, (((0,), (0,)), ((), ())), preferred_element_...  11.4 us
    all_to_all x1, blocking collectives, sent_to_all(): return lax.all_to_all(copies, axis, split_axis=0, concat_axis=0, tiled=True)  11.2 us
    unnamed x13, local copies, waits for them, and re-layouts  10.5 us
  transfers between devices with their start and end apart: 6, of which 3 were waited for; matrix products, arithmetic and copies ran while one was open for 12% of the time, Pallas kernels for 0%

commit v1 on v0

--- a/solution.py
+++ b/solution.py
@@ -118,7 +118,12 @@
     returned = lax.all_to_all(back_rows, "ctx", split_axis=0, concat_axis=0, tiled=True)
     d_merged = contract_rows(select_mat, returned).astype(jnp.bfloat16)
     chosen = columns
-    merger_grad = contract_rows(chosen, lax.all_gather(d_merged, "ctx", axis=0, tiled=True))
+    merger_grad = contract_rows(
+        chosen,
+        jnp.concatenate(
+            lax.all_to_all(jnp.stack([d_merged] * lax.axis_size("ctx")), "ctx", 0, 0), axis=0
+        ),
+    )
     return (normed, merger_grad)
 
 

time: 240 us -> 339 us (1.41)
  the two profiles are of different devices: /device:TPU:1 before, /device:TPU:12 now
where the time goes in v1:
time: 339 us; the launch traced here: 338 us
  waiting for transfers between devices  206 us (61%)
  starting transfers between devices  37.8 us (11%)
  matrix products  30.3 us (9%)
  local copies, waits for them, and re-layouts  28.1 us (8%)
  between operations  15.8 us (5%)
  blocking collectives  12.7 us (4%)
  other arithmetic  7.41 us (2%)
    all_to_all x1, waiting for transfers between devices, shards(): lax.all_to_all(jnp.stack([d_merged] * lax.axis_size('ctx')), 'ctx', 0, 0)  118 us
    psum x1, waiting for transfers between devices, shards(): lax.psum(partial_out.astype(jnp.bfloat16), 'tp').astype(jnp.float32)  70.8 us
    all_to_all x1, waiting for transfers between devices, shards(): lax.all_to_all(merged_in, 'ctx', split_axis=1, concat_axis=0, tiled=True)  16.2 us
    all_to_all x1, blocking collectives, sent_to_all(): return lax.all_to_all(copies, axis, split_axis=0, concat_axis=0, tiled=True)  12.7 us
    unnamed x13, local copies, waits for them, and re-layouts  11.9 us
    dot_general x3, matrix products, contract_rows(): lax.dot_general(left, right, (((0,), (0,)), ((), ())), preferred_element_...  9.68 us
    all_to_all x1, starting transfers between devices, shards(): lax.all_to_all(jnp.stack([d_merged] * lax.axis_size('ctx')), 'ctx', 0, 0)  8.08 us
    all_to_all x2, local copies, waits for them, and re-layouts, shards(): lax.all_to_all(merged_in, 'ctx', split_axis=1, concat_axis=0, tiled=True)  7.98 us
  transfers between devices with their start and end apart: 7, of which 3 were waited for; matrix products, arithmetic and copies ran while one was open for 9% of the time, Pallas kernels for 0%

profile of v1, /device:TPU:12, one launch (start us, length us, event | category | flops | bytes accessed | tf_op | source)
XLA Modules:
  0.0 337.7 jit_solution(16323766392405445043)
XLA Ops:
  8.1 2.1 convolution_convert_fusion.7
  10.2 2.0 convolution_convert_fusion.5
  16.3 1.6 convolution_convert_fusion
  19.9 7.5 %all-to-all-start = ((s32[32,4,1]{1,2,0:T(1,128)}), s32[32,4,1]{1,2,0:T(1,128)S(1)}, u32[]{:S(2)}, u32[]{:S(2)}) async-start(s32[32,4,1]{1,2,0:T(1,128)} %bitcast), calls=%async_computation | async-start | bytes 32768 | tf_op jit(solution)/shard_map/all_to_all | solution.py:102
  27.4 70.8 %all-reduce.2.cloned.1.call-done = bf16[512,1280]{1,0:T(8,128)(2,1)} async-done(((bf16[512,1280]{1,0:T(8,128)(2,1)}), bf16[512,1280]{1,0:T(8,128)(2,1)}) %all-reduce.2.cloned.1.call-update) | async-done | bytes 1310736 | tf_op jit(solution)/shard_map/psum | solution.py:80
  98.2 1.6 add_convert_fusion
  100.7 5.7 %convolution_convert_fusion.2 = bf16[128,1024]{1,0:T(8,128)(2,1)S(1)} fusion(bf16[128,5120]{1,0:T(8,128)(2,1)S(1)} %reshape.121, bf16[5120,1024]{1,0:T(8,128)(2,1)} %all-gather.2.cloned.1.call-done, s32[128]{0:T(128)S(1)} %compare_select_fusion), kind=kOutput, calls=%fused_computation.19 | convolution fusion | flops 1376010240 | bytes 12059136 | tf_op jit(solution)/shard_map/dot_general | solution.py:96
  107.2 7.4 %all-to-all-start.1 = ((bf16[32,4,1024]{2,1,0:T(4,128)(2,1)}), bf16[32,4,1024]{2,1,0:T(4,128)(2,1)S(1)}, u32[]{:S(2)}, u32[]{:S(2)}) async-start(bf16[32,4,1024]{2,1,0:T(4,128)(2,1)} %all_to_all.40), calls=%async_computation.1 | async-start | bytes 524288 | tf_op jit(solution)/shard_map/all_to_all | solution.py:101
  114.6 3.9 %copy.36 = bf16[1024,1024]{0,1:T(8,128)(2,1)} copy(bf16[1024,1024]{1,0:T(8,128)(2,1)} %param.13) | data formatting | bytes 4194304 | tf_op args[4]
  118.6 4.0 %copy.35 = bf16[1024,1024]{0,1:T(8,128)(2,1)} copy(bf16[1024,1024]{1,0:T(8,128)(2,1)} %param.12) | data formatting | bytes 4194304 | tf_op args[3]
  124.1 5.5 %multiply_reduce_fusion.1 = (f32[1024]{0:T(1024)S(1)}, f32[1024]{0:T(1024)S(1)}, f32[1024,1024]{0,1:T(8,128)}) fusion(bf16[1024,1024]{0,1:T(8,128)(2,1)} %copy.36, f32[1024]{0:T(1024)S(1)} %convert_element_type.78, bf16[1024,1024]{0,1:T(8,128)(2,1)} %copy.35, bf16[128,1024]{1,0:T(8,128)(2,1)S(1)} %all_to_all.42, s32[128]{0:T(128)S(1)} %eq.74, ...), kind=kOutput, calls=%fused_computation.5 | convolution fusion | flops 276953088 | bytes 8664576 | tf_op jit(solution)/shard_map/dot_general | solution.py:106
  129.7 12.7 %all_to_all.57 = f32[8,1,2048]{2,1,0:T(1,128)S(1)} all-to-all(f32[8,1,2048]{2,1,0:T(1,128)S(1)} %broadcast_in_dim.73), channel_id=1, replica_groups=mesh['ctx'=32,'tp'=8] {'tp'}, dimensions={0} | all-to-all | bytes 131072 | tf_op jit(solution)/shard_map/all_to_all | solution.py:12
  142.4 4.3 %fusion.8 = bf16[128,1024]{1,0:T(8,128)(2,1)S(1)} fusion(f32[1024,1024]{0,1:T(8,128)} %get-tuple-element.37, bf16[1024,1024]{0,1:T(8,128)(2,1)} %copy.36, f32[1024]{0:T(1024)S(1)} %get-tuple-element.34, f32[1024]{0:T(1024)S(1)} %get-tuple-element.32, f32[1024]{0:T(1024)S(1)} %get-tuple-element.33, f32[1024]{0:T(1024)S(1)} %convert_element_type.78, ...), kind=kOutput, calls=%fused_computation.17 | convolution fusion | flops 277217280 | bytes 6570496 | tf_op jit(solution)/shard_map/dot_general | solution.py:58
  147.5 7.4 %all-to-all-start.4 = ((bf16[32,4,1024]{2,1,0:T(4,128)(2,1)}), bf16[32,4,1024]{2,1,0:T(4,128)(2,1)S(1)}, u32[]{:S(2)}, u32[]{:S(2)}) async-start(bf16[32,4,1024]{2,1,0:T(4,128)(2,1)} %all_to_all.47), calls=%async_computation.4 | async-start | bytes 524288 | tf_op jit(solution)/shard_map/all_to_all | solution.py:118
  154.9 3.6 %all_to_all.44 = bf16[128,32,160]{2,1,0:T(8,128)(2,1)} reshape(bf16[512,1280]{1,0:T(8,128)(2,1)S(1)} %add_convert_fusion) | data formatting | bytes 2621440 | tf_op jit(solution)/shard_map/all_to_all | solution.py:83
  158.5 4.3 %copy.38 = bf16[128,32,160]{0,2,1:T(8,128)(2,1)} copy(bf16[128,32,160]{2,1,0:T(8,128)(2,1)} %all_to_all.44) | data formatting | bytes 2621440 | tf_op jit(solution)/shard_map/all_to_all | solution.py:83
  162.8 7.4 %all-to-all-start.3 = ((bf16[128,32,160]{0,2,1:T(8,128)(2,1)}), bf16[128,32,160]{0,2,1:T(8,128)(2,1)S(1)}, u32[]{:S(2)}, u32[]{:S(2)}) async-start(bf16[128,32,160]{0,2,1:T(8,128)(2,1)} %copy.38), calls=%async_computation.3 | async-start | bytes 2621440 | tf_op jit(solution)/shard_map/all_to_all | solution.py:83
  170.6 16.2 %all-to-all-done.3 = bf16[128,32,160]{0,2,1:T(8,128)(2,1)S(1)} async-done(((bf16[128,32,160]{0,2,1:T(8,128)(2,1)}), bf16[128,32,160]{0,2,1:T(8,128)(2,1)S(1)}, u32[]{:S(2)}, u32[]{:S(2)}) %all-to-all-start.3) | async-done | bytes 1310752 | tf_op jit(solution)/shard_map/all_to_all | solution.py:83
  186.8 4.3 %stack.2 = bf16[32,128,1024]{2,1,0:T(8,128)(2,1)} broadcast(bf16[128,1024]{1,0:T(8,128)(2,1)S(1)} %convolution_convert_fusion.1), dimensions={1,2} | broadcast | bytes 8650752 | tf_op jit(solution)/shard_map/stack | solution.py:124
  191.1 8.1 %all-to-all-start.5 = ((bf16[32,128,1024]{2,1,0:T(8,128)(2,1)}), bf16[32,128,1024]{2,1,0:T(8,128)(2,1)}, u32[]{:S(2)}, u32[]{:S(2)}) async-start(bf16[32,128,1024]{2,1,0:T(8,128)(2,1)} %stack.2), calls=%async_computation.5 | async-start | bytes 16777216 | tf_op jit(solution)/shard_map/all_to_all | solution.py:124
  199.2 3.9 %multiply_convert_fusion = bf16[1024,1024]{0,1:T(8,128)(2,1)} fusion(f32[1024,1024]{0,1:T(8,128)} %get-tuple-element.37, f32[1024]{0:T(1024)S(1)} %get-tuple-element.33, f32[1024]{0:T(1024)S(1)} %convert_element_type.78), kind=kLoop, calls=%fused_computation.2 | loop fusion | flops 3145728 | bytes 6299648 | tf_op jit(solution)/shard_map/convert_element_type | solution.py:115
  203.1 3.9 %copy.39 = bf16[1024,1024]{1,0:T(8,128)(2,1)} copy(bf16[1024,1024]{0,1:T(8,128)(2,1)} %multiply_convert_fusion) | data formatting | bytes 4194304
  207.0 118.1 %all-to-all-done.5 = bf16[32,128,1024]{2,1,0:T(8,128)(2,1)} async-done(((bf16[32,128,1024]{2,1,0:T(8,128)(2,1)}), bf16[32,128,1024]{2,1,0:T(8,128)(2,1)}, u32[]{:S(2)}, u32[]{:S(2)}) %all-to-all-start.5) | async-done | bytes 8388640 | tf_op jit(solution)/shard_map/all_to_all | solution.py:124
  325.1 5.2 %fusion.5 = f32[160,1024]{1,0:T(8,128)} fusion(bf16[32,128,1024]{2,1,0:T(8,128)(2,1)} %all-to-all-done.5, bf16[128,32,160]{0,2,1:T(8,128)(2,1)S(1)} %all-to-all-done.3), kind=kOutput, calls=%fused_computation.16 | convolution fusion | flops 1342177280 | bytes 10354688 | tf_op jit(solution)/shard_map/dot_general | solution.py:58
  (47 shorter events, 10.6 us)
Async XLA Ops:
  8.0 8.3 %copy-start = (bf16[160,1280]{1,0:T(8,128)(2,1)S(1)}, bf16[160,1280]{1,0:T(8,128)(2,1)}, u32[]{:S(2)}) copy-start(bf16[160,1280]{1,0:T(8,128)(2,1)} %param.15) | copy-start | bytes 1228804
  8.0 4.1 %copy-start.1 = (bf16[512,1280]{1,0:T(8,128)(2,1)S(1)}, bf16[512,1280]{1,0:T(8,128)(2,1)}, u32[]{:S(2)}) copy-start(bf16[512,1280]{1,0:T(8,128)(2,1)} %param.9) | copy-start | bytes 3932164
  8.0 90.2 %all-reduce.2.cloned.1.call-start = ((), (), s32[]{:S(2)}) async-start(), calls=%async_computation.6 | async-start | bytes 2621440 | tf_op jit(solution)/shard_map/psum | solution.py:80
  10.2 3.6 %copy-start.2 = (s32[512]{0:T(512)S(1)}, s32[512]{0:T(512)}, u32[]{:S(2)}) copy-start(s32[512]{0:T(512)} %param.10) | copy-start | bytes 6148
  16.2 2.2 copy-start.4
  17.9 82.8 %all-gather.2.cloned.1.call-start = ((), (), s32[]{:S(2)}) async-start(), calls=%async_computation.7 | async-start | bytes 10813440 | tf_op jit(solution)/shard_map/all_gather | solution.py:87
  19.9 87.3 %all-to-all-start = ((s32[32,4,1]{1,2,0:T(1,128)}), s32[32,4,1]{1,2,0:T(1,128)S(1)}, u32[]{:S(2)}, u32[]{:S(2)}) async-start(s32[32,4,1]{1,2,0:T(1,128)} %bitcast), calls=%async_computation | async-start | bytes 32768 | tf_op jit(solution)/shard_map/all_to_all | solution.py:102
  100.7 13.9 %copy-start.3 = (bf16[1024]{0:T(1024)(128)(2,1)S(1)}, bf16[1024]{0:T(1024)(128)(2,1)}, u32[]{:S(2)}) copy-start(bf16[1024]{0:T(1024)(128)(2,1)} %param.17) | copy-start | bytes 6148
  107.2 16.8 %all-to-all-start.1 = ((bf16[32,4,1024]{2,1,0:T(4,128)(2,1)}), bf16[32,4,1024]{2,1,0:T(4,128)(2,1)S(1)}, u32[]{:S(2)}, u32[]{:S(2)}) async-start(bf16[32,4,1024]{2,1,0:T(4,128)(2,1)} %all_to_all.40), calls=%async_computation.1 | async-start | bytes 524288 | tf_op jit(solution)/shard_map/all_to_all | solution.py:101
  147.5 15.4 %all-to-all-start.4 = ((bf16[32,4,1024]{2,1,0:T(4,128)(2,1)}), bf16[32,4,1024]{2,1,0:T(4,128)(2,1)S(1)}, u32[]{:S(2)}, u32[]{:S(2)}) async-start(bf16[32,4,1024]{2,1,0:T(4,128)(2,1)} %all_to_all.47), calls=%async_computation.4 | async-start | bytes 524288 | tf_op jit(solution)/shard_map/all_to_all | solution.py:118
  162.8 24.0 %all-to-all-start.3 = ((bf16[128,32,160]{0,2,1:T(8,128)(2,1)}), bf16[128,32,160]{0,2,1:T(8,128)(2,1)S(1)}, u32[]{:S(2)}, u32[]{:S(2)}) async-start(bf16[128,32,160]{0,2,1:T(8,128)(2,1)} %copy.38), calls=%async_computation.3 | async-start | bytes 2621440 | tf_op jit(solution)/shard_map/all_to_all | solution.py:83
  191.1 134.0 %all-to-all-start.5 = ((bf16[32,128,1024]{2,1,0:T(8,128)(2,1)}), bf16[32,128,1024]{2,1,0:T(8,128)(2,1)}, u32[]{:S(2)}, u32[]{:S(2)}) async-start(bf16[32,128,1024]{2,1,0:T(8,128)(2,1)} %stack.2), calls=%async_computation.5 | async-start | bytes 16777216 | tf_op jit(solution)/shard_map/all_to_all | solution.py:124
Sparse Core Ops, SparseCore 0:
  18.0 80.1 all-reduce.1
Sparse Core Ops, SparseCore 1:
  20.9 64.0 all-gather.1
